TPU v7x, 128 devices: a whole 4x4x4 slice. The times are simulated.
128 devices in a mesh: dp: 64 (over z_hi, x, y, core), mp: 2 (over z_lo).
Axes of the slice: x: 4, y: 4, z: 4 (z_hi: 2, z_lo: 2; z = z_hi * 2 + z_lo), core: 2. Of those that a mesh axis runs over, the one named last changes fastest.
Arguments:
- inputs: bfloat16 [8192, 1792], P('dp', 'mp'), may hold values from -6 to 6
- cotangent: bfloat16 [8192, 1792], P('dp', 'mp'), may hold values from -6 to 6
- gate_weight: bfloat16 [9472, 1792], P(('mp', 'dp')), may hold values from -0.125 to 0.125
- up_weight: bfloat16 [9472, 1792], P(('mp', 'dp')), may hold values from -0.125 to 0.125
- down_weight: bfloat16 [9472, 1792], P(('mp', 'dp')), may hold values from -0.0625 to 0.0625
Outputs:
- input_grad: bfloat16 [8192, 1792], P('dp', 'mp')
- gate_grad: bfloat16 [9472, 1792], P(('mp', 'dp'))
All inputs are finite; a program needn't handle non-finite values.
Results may differ from a plain program's by a relative error of at most 0.009.
Values may be sent and summed in bfloat16 or wider, within the bound.
A program may use at most 320 MiB of HBM per device.

v0:
```python
import jax
import jax.numpy as jnp
from jax import lax
from jax.sharding import Mesh
from jax.sharding import PartitionSpec as P

DP = ("dp_0", "dp_1", "dp_2", "dp_3")
MP_DP = ("mp", "dp_0", "dp_1", "dp_2", "dp_3")


def side_by_side(arrays, axis, dim, along):
    widths = [a.shape[along] for a in arrays]
    both = jnp.concatenate(arrays, axis=along)
    filled = lax.all_gather(both, axis, axis=dim, tiled=True)
    return tuple(jnp.split(filled, [sum(widths[:k]) for k in range(1, len(widths))], axis=along))


def split_up(x, dim, peers):
    lengths = x.shape
    pieces = x.reshape(*lengths[:dim], peers, lengths[dim] // peers, *lengths[dim + 1 :])
    return jnp.moveaxis(pieces, dim, 0)


def sent_and_summed(x, axis, dim):
    peers = lax.axis_size(axis)
    pieces = lax.all_to_all(split_up(x, dim, peers), axis, 0, 0, tiled=True)
    return jnp.sum(pieces.astype(jnp.float32), axis=0)


def in_order(pieces, dim):
    pieces = jnp.moveaxis(pieces, 0, dim)
    lengths = pieces.shape
    return pieces.reshape(*lengths[:dim], lengths[dim] * lengths[dim + 1], *lengths[dim + 2 :])


def moved_by_axis(pieces, axes, turns):
    lengths = [lax.axis_size(a) for a in axes]
    pieces = pieces.reshape(*lengths, *pieces.shape[1:])
    for k in turns:
        pieces = lax.all_to_all(pieces, axes[k], split_axis=k, concat_axis=k, tiled=True)
    return pieces.reshape(-1, *pieces.shape[len(axes) :])


def exchange_by_chip(x, groups, turns, split_dim, concat_dim):
    peers = lax.axis_size(groups[0]) * lax.axis_size(groups[1])
    pieces = split_up(x, split_dim, peers)
    return in_order(moved_by_axis(pieces, groups, turns), concat_dim)


def tdot(left, right):
    return lax.dot_general(
        left, right, (((0,), (0,)), ((), ())), preferred_element_type=jnp.float32
    )


def rdot(left, right):
    return lax.dot_general(
        left, right, (((1,), (1,)), ((), ())), preferred_element_type=jnp.float32
    )


def per_device(inputs, cotangent, gate_weight, up_weight, down_weight):
    full_in, full_cot = side_by_side((inputs, cotangent), "mp", 1, 0)
    pieces = lax.all_gather((gate_weight, up_weight), DP, axis=0, tiled=True)
    stacked = jnp.stack([rdot(full_in, pieces[0]), rdot(full_in, pieces[1])])
    gate = stacked[0]
    up = stacked[1]
    dhidden = rdot(full_cot, lax.all_gather(down_weight, DP, axis=0, tiled=True))
    sig = jax.nn.sigmoid(gate)
    act = gate * sig
    dup = (dhidden * act).astype(jnp.bfloat16)
    dgate = (dhidden * up * sig * (1.0 + gate * (1.0 - sig))).astype(jnp.bfloat16)
    owned = exchange_by_chip(dgate, (("dp_0", "dp_1", "dp_2"), "dp_3"), (1, 0), 1, 0)
    gate_sum = tdot(owned, lax.all_gather(full_in, DP, axis=0, tiled=True))
    pieces = (
        lax.all_gather(gate_weight, DP, axis=0, tiled=True),
        lax.all_gather(up_weight, DP, axis=0, tiled=True),
    )
    total = jnp.dot(dgate, pieces[0], preferred_element_type=jnp.float32)
    partial_value = total + jnp.dot(dup, pieces[1], preferred_element_type=jnp.float32)
    input_grad = sent_and_summed(partial_value.astype(jnp.bfloat16), "mp", 1).astype(jnp.bfloat16)
    gate_grad = gate_sum.astype(jnp.bfloat16)
    return (input_grad, gate_grad)


def solution(mesh):
    torus = Mesh(
        mesh.devices.reshape(2, 4, 4, 2, mesh.shape["mp"]), ("dp_0", "dp_1", "dp_2", "dp_3", "mp")
    )
    return jax.shard_map(
        per_device,
        mesh=torus,
        in_specs=(P(DP, "mp"), P(DP, "mp"), P(MP_DP, None), P(MP_DP, None), P(MP_DP, None)),
        out_specs=(P(DP, "mp"), P(MP_DP, None)),
        check_vma=False,
    )
```

profile of v0, /device:TPU:1, one launch (start us, length us, event | category | flops | bytes accessed | tf_op | source)
XLA Modules:
  0.0 530.3 jit_solution(8056646707947620844)
XLA Ops:
  7.2 0.0 all-gather.10.cloned.1.call-start
  7.2 0.7 all-gather.10.cloned.1.call-update
  7.9 0.0 all-gather.12.cloned.1.call-start
  7.9 0.7 all-gather.12.cloned.1.call-update
  8.6 0.0 all-gather.14.cloned.1.call-start
  8.7 0.7 all-gather.14.cloned.1.call-update
  9.4 0.0 all-gather.8.cloned.1.call-start
  9.4 1.1 pad_maximum_fusion
  10.5 13.4 %all_gather.17 = bf16[256,1792]{1,0:T(8,128)(2,1)S(1)} all-gather(bf16[256,896]{1,0:T(8,128)(2,1)S(1)} %pad_maximum_fusion), channel_id=1, replica_groups=mesh['dp_0'=2,'dp_1'=4,'dp_2'=4,'dp_3'=2,'mp'=2] {'mp'}, dimensions={1}, use_global_device_ids=true | all-gather | bytes 1376256 | tf_op jit(solution)/shard_map/all_gather | solution.py:14
  23.9 0.8 split.9
  24.7 0.0 all-gather.8.cloned.1.call-update
  24.7 100.6 %all-gather.10.cloned.1.call-done = bf16[64,74,1792]{2,1,0:T(8,128)(2,1)} async-done(((bf16[1,74,1792]{2,1,0:T(8,128)(2,1)}), bf16[64,74,1792]{2,1,0:T(8,128)(2,1)}) %all-gather.10.cloned.1.call-update) | async-done | bytes 16973840 | tf_op jit(solution)/shard_map/all_gather | solution.py:68
  125.3 19.3 %reshape.17 = bf16[4736,1792]{1,0:T(8,128)(2,1)} reshape(bf16[64,74,1792]{2,1,0:T(8,128)(2,1)} %all-gather.10.cloned.1.call-done) | data formatting | bytes 33947648
  144.6 92.0 %all-gather.12.cloned.1.call-done = bf16[64,74,1792]{2,1,0:T(8,128)(2,1)} async-done(((bf16[1,74,1792]{2,1,0:T(8,128)(2,1)}), bf16[64,74,1792]{2,1,0:T(8,128)(2,1)}) %all-gather.12.cloned.1.call-update) | async-done | bytes 16973840 | tf_op jit(solution)/shard_map/all_gather | solution.py:64
  236.6 19.3 %reshape.19 = bf16[4736,1792]{1,0:T(8,128)(2,1)} reshape(bf16[64,74,1792]{2,1,0:T(8,128)(2,1)} %all-gather.12.cloned.1.call-done) | data formatting | bytes 33947648
  255.9 92.0 %all-gather.14.cloned.1.call-done = bf16[64,74,1792]{2,1,0:T(8,128)(2,1)} async-done(((bf16[1,74,1792]{2,1,0:T(8,128)(2,1)}), bf16[64,74,1792]{2,1,0:T(8,128)(2,1)}) %all-gather.14.cloned.1.call-update) | async-done | bytes 16973840 | tf_op jit(solution)/shard_map/all_gather | solution.py:64
  347.9 19.4 %reshape.21 = bf16[4736,1792]{1,0:T(8,128)(2,1)} reshape(bf16[64,74,1792]{2,1,0:T(8,128)(2,1)} %all-gather.14.cloned.1.call-done) | data formatting | bytes 33947648
  367.3 12.8 %fusion.5 = f32[128,4736]{1,0:T(8,128)} fusion(bf16[4736,1792]{1,0:T(8,128)(2,1)} %reshape.17, bf16[256,1792]{1,0:T(8,128)(2,1)S(1)} %all_gather.17), kind=kOutput, calls=%fused_computation.11 | convolution fusion | flops 2172649472 | bytes 19857408 | tf_op jit(solution)/shard_map/dot_general | solution.py:57
  380.0 13.2 %fusion.8 = f32[128,4736]{1,0:T(8,128)} fusion(bf16[4736,1792]{1,0:T(8,128)(2,1)} %reshape.21, bf16[256,1792]{1,0:T(8,128)(2,1)S(1)} %all_gather.17), kind=kOutput, calls=%fused_computation.15 | convolution fusion | flops 2172649472 | bytes 19857408 | tf_op jit(solution)/shard_map/dot_general | solution.py:57
  393.3 13.2 %fusion.2 = bf16[128,4736]{1,0:T(8,128)(2,1)S(1)} fusion(f32[128,4736]{1,0:T(8,128)} %fusion.5, bf16[4736,1792]{1,0:T(8,128)(2,1)} %reshape.19, f32[128,4736]{1,0:T(8,128)} %fusion.8, bf16[256,1792]{1,0:T(8,128)(2,1)S(1)} %all_gather.17), kind=kOutput, calls=%fused_computation.3 | convolution fusion | flops 2178711552 | bytes 23494656 | tf_op jit(solution)/shard_map/dot_general | solution.py:57
  406.4 1.5 copy.10
  407.9 0.0 copy-start
  407.9 0.0 copy-start.1
  407.9 8.4 %fusion.11 = f32[128,1792]{1,0:T(8,128)S(1)} fusion(bf16[128,4736]{1,0:T(8,128)(2,1)S(1)} %fusion.2, bf16[4736,1792]{1,0:T(8,128)(2,1)} %reshape.21), kind=kOutput, calls=%fused_computation.18 | convolution fusion | flops 2172649472 | bytes 19103744 | tf_op jit(solution)/shard_map/dot_general | solution.py:79
  416.4 0.0 copy-done
  416.4 0.0 copy-done.1
  416.4 9.6 %fusion.3 = bf16[128,1792]{1,0:T(8,128)(2,1)S(1)} fusion(f32[128,1792]{1,0:T(8,128)S(1)} %fusion.11, bf16[4736,1792]{1,0:T(8,128)(2,1)} %reshape.19, f32[128,4736]{1,0:T(8,128)S(1)} %copy-done, f32[128,4736]{1,0:T(8,128)S(1)} %copy-done.1), kind=kOutput, calls=%fused_computation.7 | convolution fusion | flops 2176745472 | bytes 23199744 | tf_op jit(solution)/shard_map/dot_general | solution.py:80
  426.0 0.8 copy.16
  426.8 0.3 reshape.14
  427.2 0.5 copy.11
  427.7 4.6 all_to_all.15
  432.2 3.5 all-to-all-start
  435.7 2.4 copy.12
  438.1 11.0 %all-to-all-done = bf16[2,128,896]{2,1,0:T(8,128)(2,1)S(1)} async-done(((bf16[2,128,896]{2,1,0:T(8,128)(2,1)}), bf16[2,128,896]{2,1,0:T(8,128)(2,1)S(1)}, u32[]{:S(2)}, u32[]{:S(2)}) %all-to-all-start) | async-done | bytes 458784 | tf_op jit(solution)/shard_map/all_to_all | solution.py:26
  449.0 7.4 %all-to-all-start.2 = ((bf16[32,2,128,74]{2,1,3,0:T(2,128)(2,1)}), bf16[32,2,128,74]{2,1,3,0:T(2,128)(2,1)S(1)}, u32[]{:S(2)}, u32[]{:S(2)}) async-start(bf16[32,2,128,74]{2,1,3,0:T(2,128)(2,1)} %copy.12), calls=%async_computation.2 | async-start | bytes 2424832 | tf_op jit(solution)/shard_map/all_to_all | solution.py:40
  456.4 0.8 reduce_sum.12
  457.2 17.5 %all-to-all-done.2 = bf16[32,2,128,74]{2,1,3,0:T(2,128)(2,1)S(1)} async-done(((bf16[32,2,128,74]{2,1,3,0:T(2,128)(2,1)}), bf16[32,2,128,74]{2,1,3,0:T(2,128)(2,1)S(1)}, u32[]{:S(2)}, u32[]{:S(2)}) %all-to-all-start.2) | async-done | bytes 1212448 | tf_op jit(solution)/shard_map/all_to_all | solution.py:40
  474.7 1.3 copy.13
  476.0 0.7 reshape_reshape.3
  476.8 34.3 %all-gather.8.cloned.1.call-done = bf16[8192,1792]{1,0:T(8,128)(2,1)} async-done(((bf16[128,1792]{1,0:T(8,128)(2,1)}), bf16[8192,1792]{1,0:T(8,128)(2,1)}) %all-gather.8.cloned.1.call-update) | async-done | bytes 29360144 | tf_op jit(solution)/shard_map/all_gather | solution.py:74
  511.1 12.7 %convolution_convert_fusion = bf16[74,1792]{1,0:T(8,128)(2,1)} fusion(bf16[8192,74]{0,1:T(8,128)(2,1)S(1)} %reshape_reshape.3, bf16[8192,1792]{1,0:T(8,128)(2,1)} %all-gather.8.cloned.1.call-done), kind=kOutput, calls=%fused_computation.8 | convolution fusion | flops 2172782080 | bytes 30837760 | tf_op jit(solution)/shard_map/dot_general | solution.py:51
Async XLA Ops:
  7.2 118.1 %all-gather.10.cloned.1.call-start = ((), (), s32[]{:S(2)}) async-start(), calls=%async_computation.4 | async-start | bytes 18636800 | tf_op jit(solution)/shard_map/all_gather | solution.py:68
  7.9 228.7 %all-gather.12.cloned.1.call-start = ((), (), s32[]{:S(2)}) async-start(), calls=%async_computation.5 | async-start | bytes 18636800 | tf_op jit(solution)/shard_map/all_gather | solution.py:64
  8.6 339.2 %all-gather.14.cloned.1.call-start = ((), (), s32[]{:S(2)}) async-start(), calls=%async_computation.6 | async-start | bytes 18636800 | tf_op jit(solution)/shard_map/all_gather | solution.py:64
  9.4 501.7 %all-gather.8.cloned.1.call-start = ((), (), s32[]{:S(2)}) async-start(), calls=%async_computation.3 | async-start | bytes 29818880 | tf_op jit(solution)/shard_map/all_gather | solution.py:74
  407.9 8.4 %copy-start = (f32[128,4736]{1,0:T(8,128)S(1)}, f32[128,4736]{1,0:T(8,128)}, u32[]{:S(2)}) copy-start(f32[128,4736]{1,0:T(8,128)} %fusion.5) | copy-start | bytes 7274500
  407.9 8.4 %copy-start.1 = (f32[128,4736]{1,0:T(8,128)S(1)}, f32[128,4736]{1,0:T(8,128)}, u32[]{:S(2)}) copy-start(f32[128,4736]{1,0:T(8,128)} %fusion.8) | copy-start | bytes 7274500
  432.2 16.8 %all-to-all-start = ((bf16[2,128,896]{2,1,0:T(8,128)(2,1)}), bf16[2,128,896]{2,1,0:T(8,128)(2,1)S(1)}, u32[]{:S(2)}, u32[]{:S(2)}) async-start(bf16[2,128,896]{2,1,0:T(8,128)(2,1)} %bitcast.24), calls=%async_computation | async-start | bytes 917504 | tf_op jit(solution)/shard_map/all_to_all | solution.py:26
  449.0 25.7 %all-to-all-start.2 = ((bf16[32,2,128,74]{2,1,3,0:T(2,128)(2,1)}), bf16[32,2,128,74]{2,1,3,0:T(2,128)(2,1)S(1)}, u32[]{:S(2)}, u32[]{:S(2)}) async-start(bf16[32,2,128,74]{2,1,3,0:T(2,128)(2,1)} %copy.12), calls=%async_computation.2 | async-start | bytes 2424832 | tf_op jit(solution)/shard_map/all_to_all | solution.py:40
Sparse Core Ops, SparseCore 0:
  11.1 114.1 all-gather.9
  128.4 108.1 all-gather.11
  239.7 108.1 all-gather.13
  350.9 160.2 all-gather.7
where the time goes:
time: 532 us; the launch traced here: 530 us
  waiting for transfers between devices  349 us (66%)
  matrix products  69.9 us (13%)
  local copies, waits for them, and re-layouts  66.4 us (12%)
  blocking collectives  17.9 us (3%)
  between operations  13.9 us (3%)
  starting transfers between devices  11 us (2%)
    all_gather x2, waiting for transfers between devices, per_device(): pieces = lax.all_gather((gate_weight, up_weight), DP, axis=0, tiled=True)  184 us
    all_gather x1, waiting for transfers between devices, per_device(): lax.all_gather(down_weight, DP, axis=0, tiled=True)  101 us
    unnamed x7, local copies, waits for them, and re-layouts  58 us
    dot_general x3, matrix products, rdot(): lax.dot_general(left, right, (((1,), (1,)), ((), ())), preferred_element_...  39.2 us
    all_gather x1, waiting for transfers between devices, per_device(): gate_sum = tdot(owned, lax.all_gather(full_in, DP, axis=0, tiled=True))  34.3 us
    all_to_all x1, waiting for transfers between devices, moved_by_axis(): lax.all_to_all(pieces, axes[k], split_axis=k, concat_axis=k, tiled=True)  17.5 us
    all_gather x1, blocking collectives, side_by_side(): filled = lax.all_gather(both, axis, axis=dim, tiled=True)  13.4 us
    dot_general x1, matrix products, tdot(): lax.dot_general(left, right, (((0,), (0,)), ((), ())), preferred_element_...  12.7 us
  transfers between devices with their start and end apart: 6, of which 6 were waited for; matrix products, arithmetic and copies ran while one was open for 24% of the time, Pallas kernels for 0%

commit v1 on v0

--- a/solution.py
+++ b/solution.py
@@ -65,7 +65,15 @@
     stacked = jnp.stack([rdot(full_in, pieces[0]), rdot(full_in, pieces[1])])
     gate = stacked[0]
     up = stacked[1]
-    dhidden = rdot(full_cot, lax.all_gather(down_weight, DP, axis=0, tiled=True))
+
+    def _switch_knots(u_in, axis_tag):
+        ledger = []
+        for _ in range(jax.lax.axis_size(axis_tag)):
+            ledger.append(u_in)
+        prior = jnp.concatenate(jax.lax.all_to_all(jnp.stack(ledger), axis_tag, 0, 0), 0)
+        return prior
+
+    dhidden = rdot(full_cot, _switch_knots(down_weight, DP))
     sig = jax.nn.sigmoid(gate)
     act = gate * sig
     dup = (dhidden * act).astype(jnp.bfloat16)

time: 532 us -> 604 us (1.14)
  blocking collectives: 17.9 us -> 247 us
  waiting for transfers between devices: 349 us -> 193 us
    all_to_all x0 -> x1, blocking collectives: none -> 229 us  [_switch_knots(): jax.lax.all_to_all(jnp.stack(ledger), axis_tag, 0, 0)]
    all_gather x1 -> x0, waiting for transfers between devices: 101 us -> none  [per_device(): lax.all_gather(down_weight, DP, axis=0, tiled=True)]
    all_gather x2, waiting for transfers between devices: 184 us -> 114 us  [per_device(): pieces = lax.all_gather((gate_weight, up_weight), DP, axis=0, tiled=True)]
    reshape x0 -> x1, local copies, waits for them, and re-layouts: none -> 19.5 us  [_switch_knots(): jnp.concatenate(jax.lax.all_to_all(jnp.stack(ledger), axis_tag, 0, 0), 0)]
    unnamed x7 -> x8, local copies, waits for them, and re-layouts: 58 us -> 38.7 us
    all_gather x1, waiting for transfers between devices: 34.3 us -> 50.4 us  [per_device(): gate_sum = tdot(owned, lax.all_gather(full_in, DP, axis=0, tiled=True))]
  transfers between devices with their start and end apart: 6 -> 5, of which waited for: 6 -> 5; matrix products, arithmetic and copies ran while one was open for 24% -> 21% of each run, Pallas kernels for 0% -> 0%
where the time goes in v1:
time: 604 us; the launch traced here: 602 us
  blocking collectives  247 us (41%)
  waiting for transfers between devices  193 us (32%)
  matrix products  69.1 us (11%)
  local copies, waits for them, and re-layouts  68 us (11%)
  between operations  13.9 us (2%)
  starting transfers between devices  8.61 us (1%)
    all_to_all x1, blocking collectives, _switch_knots(): jax.lax.all_to_all(jnp.stack(ledger), axis_tag, 0, 0)  229 us
    all_gather x2, waiting for transfers between devices, per_device(): pieces = lax.all_gather((gate_weight, up_weight), DP, axis=0, tiled=True)  114 us
    all_gather x1, waiting for transfers between devices, per_device(): gate_sum = tdot(owned, lax.all_gather(full_in, DP, axis=0, tiled=True))  50.4 us
    dot_general x3, matrix products, rdot(): lax.dot_general(left, right, (((1,), (1,)), ((), ())), preferred_element_...  39.1 us
    unnamed x8, local copies, waits for them, and re-layouts  38.7 us
    reshape x1, local copies, waits for them, and re-layouts, _switch_knots(): jnp.concatenate(jax.lax.all_to_all(jnp.stack(ledger), axis_tag, 0, 0), 0)  19.5 us
    all_to_all x1, waiting for transfers between devices, moved_by_axis(): lax.all_to_all(pieces, axes[k], split_axis=k, concat_axis=k, tiled=True)  17.5 us
    all_gather x1, blocking collectives, side_by_side(): filled = lax.all_gather(both, axis, axis=dim, tiled=True)  13.4 us
  transfers between devices with their start and end apart: 5, of which 5 were waited for; matrix products, arithmetic and copies ran while one was open for 21% of the time, Pallas kernels for 0%

profile of v1, /device:TPU:1, one launch (start us, length us, event | category | flops | bytes accessed | tf_op | source)
XLA Modules:
  0.0 602.3 jit_solution(5598862981649085335)
XLA Ops:
  7.2 0.0 copy-start.2
  7.2 0.0 all-gather.8.cloned.1.call-start
  7.2 0.7 all-gather.8.cloned.1.call-update
  7.9 0.0 all-gather.10.cloned.1.call-start
  8.0 0.7 all-gather.10.cloned.1.call-update
  8.7 0.0 all-gather.6.cloned.1.call-start
  8.7 1.1 pad_maximum_fusion
  9.8 13.4 %all_gather.14 = bf16[256,1792]{1,0:T(8,128)(2,1)S(1)} all-gather(bf16[256,896]{1,0:T(8,128)(2,1)S(1)} %pad_maximum_fusion), channel_id=1, replica_groups=mesh['dp_0'=2,'dp_1'=4,'dp_2'=4,'dp_3'=2,'mp'=2] {'mp'}, dimensions={1}, use_global_device_ids=true | all-gather | bytes 1376256 | tf_op jit(solution)/shard_map/all_gather | solution.py:14
  23.2 0.8 split.9
  24.0 0.0 all-gather.6.cloned.1.call-update
  24.0 0.0 copy-done.2
  24.0 1.6 stack.2
  25.6 228.7 %all_to_all.20 = bf16[64,74,1792]{2,1,0:T(8,128)(2,1)} all-to-all(bf16[64,74,1792]{2,1,0:T(8,128)(2,1)S(1)} %stack.2), channel_id=1, replica_groups=mesh['dp_0'=2,'dp_1'=4,'dp_2'=4,'dp_3'=2,'mp'=2] {'dp_0','dp_1','dp_2','..., dimensions={0} | all-to-all | bytes 33947648 | tf_op jit(solution)/shard_map/all_to_all | solution.py:73
  254.2 19.5 %reshape.18 = bf16[4736,1792]{1,0:T(8,128)(2,1)} reshape(bf16[64,74,1792]{2,1,0:T(8,128)(2,1)} %all_to_all.20) | data formatting | bytes 33947648 | tf_op jit(solution)/shard_map/reshape | solution.py:73
  273.7 13.0 %fusion.5 = f32[128,4736]{1,0:T(8,128)} fusion(bf16[4736,1792]{1,0:T(8,128)(2,1)} %reshape.18, bf16[256,1792]{1,0:T(8,128)(2,1)S(1)} %all_gather.14), kind=kOutput, calls=%fused_computation.11 | convolution fusion | flops 2172649472 | bytes 19857408 | tf_op jit(solution)/shard_map/dot_general | solution.py:57
  286.7 21.1 %all-gather.8.cloned.1.call-done = bf16[64,74,1792]{2,1,0:T(8,128)(2,1)} async-done(((bf16[1,74,1792]{2,1,0:T(8,128)(2,1)}), bf16[64,74,1792]{2,1,0:T(8,128)(2,1)}) %all-gather.8.cloned.1.call-update) | async-done | bytes 16973840 | tf_op jit(solution)/shard_map/all_gather | solution.py:64
  307.7 19.3 %reshape.23 = bf16[4736,1792]{1,0:T(8,128)(2,1)} reshape(bf16[64,74,1792]{2,1,0:T(8,128)(2,1)} %all-gather.8.cloned.1.call-done) | data formatting | bytes 33947648
  327.1 92.6 %all-gather.10.cloned.1.call-done = bf16[64,74,1792]{2,1,0:T(8,128)(2,1)} async-done(((bf16[1,74,1792]{2,1,0:T(8,128)(2,1)}), bf16[64,74,1792]{2,1,0:T(8,128)(2,1)}) %all-gather.10.cloned.1.call-update) | async-done | bytes 16973840 | tf_op jit(solution)/shard_map/all_gather | solution.py:64
  419.7 19.3 %reshape.25 = bf16[4736,1792]{1,0:T(8,128)(2,1)} reshape(bf16[64,74,1792]{2,1,0:T(8,128)(2,1)} %all-gather.10.cloned.1.call-done) | data formatting | bytes 33947648
  439.0 12.8 %fusion.8 = f32[128,4736]{1,0:T(8,128)} fusion(bf16[4736,1792]{1,0:T(8,128)(2,1)} %reshape.25, bf16[256,1792]{1,0:T(8,128)(2,1)S(1)} %all_gather.14), kind=kOutput, calls=%fused_computation.15 | convolution fusion | flops 2172649472 | bytes 19857408 | tf_op jit(solution)/shard_map/dot_general | solution.py:57
  451.8 13.3 %fusion.2 = bf16[128,4736]{1,0:T(8,128)(2,1)S(1)} fusion(f32[128,4736]{1,0:T(8,128)} %fusion.5, bf16[4736,1792]{1,0:T(8,128)(2,1)} %reshape.23, f32[128,4736]{1,0:T(8,128)} %fusion.8, bf16[256,1792]{1,0:T(8,128)(2,1)S(1)} %all_gather.14), kind=kOutput, calls=%fused_computation.3 | convolution fusion | flops 2178711552 | bytes 23494656 | tf_op jit(solution)/shard_map/dot_general | solution.py:57
  465.1 1.5 copy.10
  466.6 0.0 copy-start
  466.6 0.0 copy-start.1
  466.6 8.8 %fusion.11 = f32[128,1792]{1,0:T(8,128)S(1)} fusion(bf16[128,4736]{1,0:T(8,128)(2,1)S(1)} %fusion.2, bf16[4736,1792]{1,0:T(8,128)(2,1)} %reshape.25), kind=kOutput, calls=%fused_computation.18 | convolution fusion | flops 2172649472 | bytes 19103744 | tf_op jit(solution)/shard_map/dot_general | solution.py:87
  475.4 0.0 copy-done
  475.4 0.0 copy-done.1
  475.5 8.6 %fusion.3 = bf16[128,1792]{1,0:T(8,128)(2,1)S(1)} fusion(f32[128,1792]{1,0:T(8,128)S(1)} %fusion.11, bf16[4736,1792]{1,0:T(8,128)(2,1)} %reshape.23, f32[128,4736]{1,0:T(8,128)S(1)} %copy-done, f32[128,4736]{1,0:T(8,128)S(1)} %copy-done.1), kind=kOutput, calls=%fused_computation.7 | convolution fusion | flops 2176745472 | bytes 23199744 | tf_op jit(solution)/shard_map/dot_general | solution.py:88
  484.0 0.8 copy.16
  484.8 0.3 reshape.20
  485.2 0.5 copy.11
  485.7 5.4 all_to_all.21
  491.1 3.5 all-to-all-start.1
  494.6 2.3 copy.12
  496.8 10.4 %all-to-all-done.1 = bf16[2,128,896]{2,1,0:T(8,128)(2,1)S(1)} async-done(((bf16[2,128,896]{2,1,0:T(8,128)(2,1)}), bf16[2,128,896]{2,1,0:T(8,128)(2,1)S(1)}, u32[]{:S(2)}, u32[]{:S(2)}) %all-to-all-start.1) | async-done | bytes 458784 | tf_op jit(solution)/shard_map/all_to_all | solution.py:26
  507.3 5.0 all-to-all-start.3
  512.3 0.8 reduce_sum.12
  513.1 17.5 %all-to-all-done.3 = bf16[32,2,128,74]{2,1,3,0:T(2,128)(2,1)S(1)} async-done(((bf16[32,2,128,74]{2,1,3,0:T(2,128)(2,1)}), bf16[32,2,128,74]{2,1,3,0:T(2,128)(2,1)S(1)}, u32[]{:S(2)}, u32[]{:S(2)}) %all-to-all-start.3) | async-done | bytes 1212448 | tf_op jit(solution)/shard_map/all_to_all | solution.py:40
  530.6 1.3 copy.13
  531.9 0.7 reshape_reshape.3
  532.7 50.4 %all-gather.6.cloned.1.call-done = bf16[8192,1792]{1,0:T(8,128)(2,1)} async-done(((bf16[128,1792]{1,0:T(8,128)(2,1)}), bf16[8192,1792]{1,0:T(8,128)(2,1)}) %all-gather.6.cloned.1.call-update) | async-done | bytes 29360144 | tf_op jit(solution)/shard_map/all_gather | solution.py:82
  583.0 12.7 %convolution_convert_fusion = bf16[74,1792]{1,0:T(8,128)(2,1)} fusion(bf16[8192,74]{0,1:T(8,128)(2,1)S(1)} %reshape_reshape.3, bf16[8192,1792]{1,0:T(8,128)(2,1)} %all-gather.6.cloned.1.call-done), kind=kOutput, calls=%fused_computation.8 | convolution fusion | flops 2172782080 | bytes 30837760 | tf_op jit(solution)/shard_map/dot_general | solution.py:51
Async XLA Ops:
  7.2 16.8 %copy-start.2 = (bf16[74,1792]{1,0:T(8,128)(2,1)S(1)}, bf16[74,1792]{1,0:T(8,128)(2,1)}, u32[]{:S(2)}) copy-start(bf16[74,1792]{1,0:T(8,128)(2,1)} %param.9) | copy-start | bytes 795652
  7.2 300.6 %all-gather.8.cloned.1.call-start = ((), (), s32[]{:S(2)}) async-start(), calls=%async_computation.5 | async-start | bytes 18636800 | tf_op jit(solution)/shard_map/all_gather | solution.py:64
  7.9 411.8 %all-gather.10.cloned.1.call-start = ((), (), s32[]{:S(2)}) async-start(), calls=%async_computation.6 | async-start | bytes 18636800 | tf_op jit(solution)/shard_map/all_gather | solution.py:64
  8.7 574.4 %all-gather.6.cloned.1.call-start = ((), (), s32[]{:S(2)}) async-start(), calls=%async_computation.4 | async-start | bytes 29818880 | tf_op jit(solution)/shard_map/all_gather | solution.py:82
  466.6 8.8 %copy-start = (f32[128,4736]{1,0:T(8,128)S(1)}, f32[128,4736]{1,0:T(8,128)}, u32[]{:S(2)}) copy-start(f32[128,4736]{1,0:T(8,128)} %fusion.5) | copy-start | bytes 7274500
  466.6 8.8 %copy-start.1 = (f32[128,4736]{1,0:T(8,128)S(1)}, f32[128,4736]{1,0:T(8,128)}, u32[]{:S(2)}) copy-start(f32[128,4736]{1,0:T(8,128)} %fusion.8) | copy-start | bytes 7274500
  491.1 16.2 %all-to-all-start.1 = ((bf16[2,128,896]{2,1,0:T(8,128)(2,1)}), bf16[2,128,896]{2,1,0:T(8,128)(2,1)S(1)}, u32[]{:S(2)}, u32[]{:S(2)}) async-start(bf16[2,128,896]{2,1,0:T(8,128)(2,1)} %bitcast.23), calls=%async_computation.1 | async-start | bytes 917504 | tf_op jit(solution)/shard_map/all_to_all | solution.py:26
  507.3 23.3 %all-to-all-start.3 = ((bf16[32,2,128,74]{2,1,3,0:T(2,128)(2,1)}), bf16[32,2,128,74]{2,1,3,0:T(2,128)(2,1)S(1)}, u32[]{:S(2)}, u32[]{:S(2)}) async-start(bf16[32,2,128,74]{2,1,3,0:T(2,128)(2,1)} %copy.12), calls=%async_computation.3 | async-start | bytes 2424832 | tf_op jit(solution)/shard_map/all_to_all | solution.py:40
Sparse Core Ops, SparseCore 0:
  11.1 296.6 all-gather.7
  310.9 108.7 all-gather.9
  422.8 160.2 all-gather.5
